TPU v7x, 32 devices: a whole 2x2x4 slice. The times are simulated.
32 devices in a mesh: groups: 2 (over x), ctx: 16 (over z, y, core).
Axes of the slice: x: 2, y: 2, z: 4, core: 2. Of those that a mesh axis runs over, the one named last changes fastest.
Arguments:
- queries: bfloat16 [128, 8192], P(('groups', 'ctx')), parts along dimension 0, may hold values from -200 to 200
- new_kv: bfloat16 [128, 1024], P(('groups', 'ctx')), parts along dimension 0, may hold values from -9 to 9
- prefix_cache: bfloat16 [32768, 1024], P(('groups', 'ctx')), parts along dimension 0, may hold values from -6.5 to 6.5
- positions: int32 [128], P('groups'), parts along dimension 0, may hold values from 0 to 63, each once
- lengths: int32 [32], P('groups'), parts along dimension 0, may hold values from 1 to 1024, 12288 in all
- out_weight: bfloat16 [8192, 16384], P(None, 'ctx'), may hold values from -0.0625 to 0.0625
Outputs:
- attended: bfloat16 [128, 8192], P(('groups', 'ctx')), parts along dimension 0
- projected: bfloat16 [128, 16384], P('groups', 'ctx'), parts along dimension 0
There are 2 independent parts, one for each index of `groups`. A program takes and returns all parts, laid end to end along the dimension named above; an argument that names none is the same for every part. Nothing has to cross between parts.
Inputs may be any that keep to these rules, and one draw needn't show every extreme that they name: `positions`: a permutation of 0 to 63. The filled slots of shard i are its first lengths[i] slots; they sum to 12288, and some shard is full.
All inputs are finite; a program needn't handle non-finite values.
Results may differ from a plain program's by a relative error of at most 0.0045.
Values may be sent and summed in bfloat16 or wider, within the bound.
A program may use at most 128 MiB of HBM per device.

v0:
```python
import math

import jax
import jax.numpy as jnp
from jax import lax
from jax.sharding import PartitionSpec as P

HQ = 64
KVH = 4
HD = 128
BLK = 256


very_low = -1e30


def block_stats(rows_q, key_rows, values, live_mask, score_scale):
    scores = (
        jnp.einsum("rd,kd->rk", rows_q, key_rows, preferred_element_type=jnp.float32) * score_scale
    )
    scores = jnp.where(live_mask, scores, very_low)
    row_max = jnp.max(scores, axis=1)
    weights = jnp.where(live_mask, jnp.exp(scores - row_max[:, None]), 0.0)
    row_total = jnp.sum(weights, axis=1)
    summed = jnp.dot(weights.astype(jnp.bfloat16), values, preferred_element_type=jnp.float32)
    return (row_max, summed, row_total)


def fold_stats(running, fresh):
    old_max, old_sum, old_total = running
    new_max, new_sum, new_total = fresh
    joint_max = jnp.maximum(old_max, new_max)
    keep_old = jnp.exp(old_max - joint_max)
    keep_new = jnp.exp(new_max - joint_max)
    return (
        joint_max,
        old_sum * keep_old[..., None] + new_sum * keep_new[..., None],
        old_total * keep_old + new_total * keep_new,
    )


def shards(queries, new_kv, prefix_cache, positions, lengths, out_weight):
    ctx_size = lax.axis_size("ctx")
    my_index = lax.axis_index("ctx")
    tok_dev = queries.shape[0]
    turn_count = tok_dev * ctx_size
    per_group = HQ // KVH
    all_rows = turn_count * per_group
    score_scale = 1.0 / math.sqrt(HD)
    all_queries, all_kv = (
        lax.all_gather(queries, "ctx", axis=0, tiled=True),
        lax.all_gather(new_kv, "ctx", axis=0, tiled=True),
    )
    query_groups = all_queries.reshape(turn_count, KVH, per_group, HD)
    group_rows = [query_groups[:, group_index].reshape(all_rows, HD) for group_index in range(KVH)]
    cache_view = prefix_cache.reshape(-1, KVH, 2, HD)
    slot_count = cache_view.shape[0]
    my_length = lax.dynamic_index_in_dim(lengths, my_index, 0, keepdims=False)
    start_state = (
        jnp.full((KVH, all_rows), very_low, jnp.float32),
        jnp.zeros((KVH, all_rows, HD), jnp.float32),
        jnp.zeros((KVH, all_rows), jnp.float32),
    )

    def visit_block(block_index, running):
        first_slot = block_index * BLK
        cache_piece = lax.dynamic_slice_in_dim(cache_view, first_slot, BLK, 0)
        live_slots = (first_slot + jnp.arange(BLK, dtype=jnp.int32) < my_length)[None, :]
        max_list, sum_list, total_list = ([], [], [])
        for group_index in range(KVH):
            fresh = block_stats(
                group_rows[group_index],
                cache_piece[:, group_index, 0],
                cache_piece[:, group_index, 1],
                live_slots,
                score_scale,
            )
            merged = fold_stats(
                (running[0][group_index], running[1][group_index], running[2][group_index]), fresh
            )
            max_list.append(merged[0])
            sum_list.append(merged[1])
            total_list.append(merged[2])
        return (jnp.stack(max_list), jnp.stack(sum_list), jnp.stack(total_list))

    running = lax.fori_loop(0, slot_count // BLK, visit_block, start_state)
    own_groups = queries.reshape(tok_dev, KVH, per_group, HD)
    kv_view = all_kv.reshape(turn_count, KVH, 2, HD)
    own_positions = lax.dynamic_slice_in_dim(positions, my_index * tok_dev, tok_dev, 0)
    causal = jnp.repeat(own_positions[:, None] >= positions[None, :], per_group, axis=0)
    new_stats = [
        block_stats(
            own_groups[:, group_index].reshape(tok_dev * per_group, HD),
            kv_view[:, group_index, 0],
            kv_view[:, group_index, 1],
            causal,
            score_scale,
        )
        for group_index in range(KVH)
    ]
    new_max = jnp.stack([entry[0] for entry in new_stats]).reshape(KVH, tok_dev, per_group)
    new_sum = jnp.stack([entry[1] for entry in new_stats]).reshape(KVH, tok_dev, per_group, HD)
    new_total = jnp.stack([entry[2] for entry in new_stats]).reshape(KVH, tok_dev, per_group)
    prefix_max = running[0].reshape(KVH, turn_count, per_group)
    prefix_sum = running[1].reshape(KVH, turn_count, per_group, HD)
    prefix_total = running[2].reshape(KVH, turn_count, per_group)
    got_max, got_sum, got_total = (
        lax.all_to_all(prefix_max[None], "ctx", split_axis=2, concat_axis=0, tiled=True),
        lax.all_to_all(prefix_sum[None], "ctx", split_axis=2, concat_axis=0, tiled=True),
        lax.all_to_all(prefix_total[None], "ctx", split_axis=2, concat_axis=0, tiled=True),
    )
    joint_max = jnp.max(got_max, axis=0)
    weight = jnp.exp(got_max - joint_max[None])
    merged = (
        joint_max,
        jnp.sum(got_sum * weight[..., None], axis=0),
        jnp.sum(got_total * weight, axis=0),
    )
    combined = fold_stats(merged, (new_max, new_sum, new_total))
    result = combined[1] / combined[2][..., None]
    attended = result.transpose(1, 0, 2, 3).reshape(tok_dev, HQ * HD).astype(jnp.bfloat16)
    projected = jnp.dot(
        lax.all_gather(attended, "ctx", axis=0, tiled=True),
        out_weight,
        preferred_element_type=jnp.float32,
    ).astype(jnp.bfloat16)
    return (attended, projected)


def solution(mesh):
    in_specs = (
        P(("groups", "ctx"), None),
        P(("groups", "ctx"), None),
        P(("groups", "ctx"), None),
        P("groups"),
        P("groups"),
        P(None, "ctx"),
    )
    out_specs = (P(("groups", "ctx"), None), P("groups", "ctx"))
    return jax.shard_map(shards, mesh=mesh, in_specs=in_specs, out_specs=out_specs, check_vma=False)
```

profile of v0, /device:TPU:0, one launch (start us, length us, event | category | flops | bytes accessed | tf_op | source)
XLA Modules:
  0.0 246.9 jit_solution(8308737330803079454)
XLA Ops:
  7.9 4.0 %copy.109 = bf16[1024,1024]{0,1:T(8,128)(2,1)} copy(bf16[1024,1024]{1,0:T(8,128)(2,1)} %param.10) | data formatting | bytes 4194304 | tf_op args[2]
  12.5 38.3 %all-gather.6.cloned.1.call-done = bf16[16,4,8192]{2,1,0:T(4,128)(2,1)} async-done(((bf16[1,4,8192]{2,1,0:T(4,128)(2,1)}), bf16[16,4,8192]{2,1,0:T(4,128)(2,1)}) %all-gather.6.cloned.1.call-update) | async-done | bytes 1048592 | tf_op jit(solution)/shard_map/all_gather | solution.py:51
  50.8 2.1 reshape.407
  53.3 49.2 %while.17 = (s32[]{:T(128)}, f32[4,1024]{1,0:T(4,128)S(1)}, f32[4,1024,128]{2,1,0:T(8,128)S(1)}, f32[4,1024]{1,0:T(4,128)S(1)}, s32[]{:T(128)}, /*index=5*/bf16[...) while((s32[]{:T(128)}, f32[4,1024]{1,0:T(4,128)S(1)}, ...), condition=%wide.region_9.10_spmd, body=%wide.region_0.9_spmd.sunk | while | flops 549508608 | bytes 22911804 | solution.py:86
  59.6 1.4 fusion.148
  61.1 1.4 fusion.150
  72.0 1.4 fusion.148
  73.4 1.4 fusion.150
  74.8 1.4 fusion.152
  84.3 1.4 fusion.148
  85.7 1.4 fusion.150
  87.1 1.4 fusion.152
  96.6 1.4 fusion.148
  98.0 1.4 fusion.150
  99.5 1.4 fusion.152
  103.5 3.7 %all-to-all-start.2 = ((f32[16,1,256]{2,1,0:T(1,128)}), f32[16,1,256]{2,1,0:T(1,128)S(1)}, u32[]{:S(2)}, u32[]{:S(2)}) async-start(f32[16,1,256]{2,1,0:T(1,128)} %reshape.430), calls=%async_computation.2 | async-start | bytes 32768 | tf_op jit(solution)/shard_map/all_to_all | solution.py:110
  108.1 5.6 %all-to-all-done.2 = f32[16,1,256]{2,1,0:T(1,128)S(1)} async-done(((f32[16,1,256]{2,1,0:T(1,128)}), f32[16,1,256]{2,1,0:T(1,128)S(1)}, u32[]{:S(2)}, u32[]{:S(2)}) %all-to-all-start.2) | async-done | bytes 16416 | tf_op jit(solution)/shard_map/all_to_all | solution.py:110
  113.7 3.5 %all-to-all-start.1 = ((f32[16,1,256]{2,1,0:T(1,128)}), f32[16,1,256]{2,1,0:T(1,128)S(1)}, u32[]{:S(2)}, u32[]{:S(2)}) async-start(f32[16,1,256]{2,1,0:T(1,128)} %reshape.428), calls=%async_computation.1 | async-start | bytes 32768 | tf_op jit(solution)/shard_map/all_to_all | solution.py:108
  117.2 1.7 copy.111
  118.8 4.8 %all-to-all-done.1 = f32[16,1,256]{2,1,0:T(1,128)S(1)} async-done(((f32[16,1,256]{2,1,0:T(1,128)}), f32[16,1,256]{2,1,0:T(1,128)S(1)}, u32[]{:S(2)}, u32[]{:S(2)}) %all-to-all-start.1) | async-done | bytes 16416 | tf_op jit(solution)/shard_map/all_to_all | solution.py:108
  123.6 3.7 %all-to-all-start = ((f32[1,4,64,16,128]{4,3,1,0,2:T(8,128)}), f32[1,4,64,16,128]{4,3,1,0,2:T(8,128)S(1)}, u32[]{:S(2)}, u32[]{:S(2)}) async-start(f32[1,4,64,16,128]{4,3,1,0,2:T(8,128)} %copy.111), calls=%async_computation | async-start | bytes 4194304 | tf_op jit(solution)/shard_map/all_to_all | solution.py:109
  127.7 50.6 %all-gather.1 = bf16[16,4,1024]{2,1,0:T(4,128)(2,1)S(1)} all-gather(bf16[1,4,1024]{2,1,0:T(4,128)(2,1)S(1)} %bitcast.302), channel_id=1, replica_groups=mesh['groups'=2,'ctx'=16] {'ctx'}, dimensions={0}, use_global_device_ids=true | all-gather | bytes 139264 | tf_op jit(solution)/shard_map/all_gather | solution.py:52
  185.5 43.8 %all-gather.8.cloned.1.call-done = bf16[16,4,8192]{2,1,0:T(4,128)(2,1)} async-done(((bf16[1,4,8192]{2,1,0:T(4,128)(2,1)}), bf16[16,4,8192]{2,1,0:T(4,128)(2,1)}) %all-gather.8.cloned.1.call-update) | async-done | bytes 1048592 | tf_op jit(solution)/shard_map/all_gather | solution.py:123
  230.6 9.4 %convolution_convert_fusion = bf16[64,1024]{1,0:T(8,128)(2,1)} fusion(bf16[64,8192]{1,0:T(8,128)(2,1)S(1)} %reshape.420, bf16[8192,1024]{1,0:T(8,128)(2,1)} %param.13), kind=kOutput, calls=%fused_computation.97 | convolution fusion | flops 1073807360 | bytes 17956864 | tf_op jit(solution)/shard_map/dot_general | solution.py:122
  (131 shorter events, 45.3 us)
Async XLA Ops:
  7.2 43.6 %all-gather.6.cloned.1.call-start = ((), (), s32[]{:S(2)}) async-start(), calls=%async_computation.3 | async-start | bytes 1114112 | tf_op jit(solution)/shard_map/all_gather | solution.py:51
  7.9 4.0 %copy-start.2 = (s32[16]{0:T(128)S(1)}, s32[16]{0:T(128)}, u32[]{:S(2)}) copy-start(s32[16]{0:T(128)} %param.12) | copy-start | bytes 196
  103.5 10.2 %all-to-all-start.2 = ((f32[16,1,256]{2,1,0:T(1,128)}), f32[16,1,256]{2,1,0:T(1,128)S(1)}, u32[]{:S(2)}, u32[]{:S(2)}) async-start(f32[16,1,256]{2,1,0:T(1,128)} %reshape.430), calls=%async_computation.2 | async-start | bytes 32768 | tf_op jit(solution)/shard_map/all_to_all | solution.py:110
  113.7 10.0 %all-to-all-start.1 = ((f32[16,1,256]{2,1,0:T(1,128)}), f32[16,1,256]{2,1,0:T(1,128)S(1)}, u32[]{:S(2)}, u32[]{:S(2)}) async-start(f32[16,1,256]{2,1,0:T(1,128)} %reshape.428), calls=%async_computation.1 | async-start | bytes 32768 | tf_op jit(solution)/shard_map/all_to_all | solution.py:108
  118.8 8.6 %copy-start.3 = (s32[64]{0:T(128)S(1)}, s32[64]{0:T(128)}, u32[]{:S(2)}) copy-start(s32[64]{0:T(128)} %param.11) | copy-start | bytes 772
  118.8 8.9 %copy-start = (bf16[4,8192]{1,0:T(4,128)(2,1)S(1)}, bf16[4,8192]{1,0:T(4,128)(2,1)}, u32[]{:S(2)}) copy-start(bf16[4,8192]{1,0:T(4,128)(2,1)} %param.8) | copy-start | bytes 196612
  118.8 8.9 %copy-start.1 = (bf16[4,1024]{1,0:T(4,128)(2,1)S(1)}, bf16[4,1024]{1,0:T(4,128)(2,1)}, u32[]{:S(2)}) copy-start(bf16[4,1024]{1,0:T(4,128)(2,1)} %param.9) | copy-start | bytes 24580
  123.6 59.6 %all-to-all-start = ((f32[1,4,64,16,128]{4,3,1,0,2:T(8,128)}), f32[1,4,64,16,128]{4,3,1,0,2:T(8,128)S(1)}, u32[]{:S(2)}, u32[]{:S(2)}) async-start(f32[1,4,64,16,128]{4,3,1,0,2:T(8,128)} %copy.111), calls=%async_computation | async-start | bytes 4194304 | tf_op jit(solution)/shard_map/all_to_all | solution.py:109
  127.4 102.0 %all-gather.8.cloned.1.call-start = ((), (), s32[]{:S(2)}) async-start(), calls=%async_computation.4 | async-start | bytes 1114112 | tf_op jit(solution)/shard_map/all_gather | solution.py:123
Sparse Core Ops, SparseCore 0:
  10.1 40.5 all-gather.5
  184.9 44.3 all-gather.7
where the time goes:
time: 249 us; the launch traced here: 247 us
  waiting for transfers between devices  93.1 us (37%)
  matrix products  52.2 us (21%)
  blocking collectives  50.6 us (20%)
  local copies, waits for them, and re-layouts  15.5 us (6%)
  between operations  14.4 us (6%)
  starting transfers between devices  11 us (4%)
  other arithmetic  9.62 us (4%)
    all_gather x1, blocking collectives, shards(): lax.all_gather(new_kv, 'ctx', axis=0, tiled=True)  50.6 us
    all_gather x1, waiting for transfers between devices, shards(): lax.all_gather(attended, 'ctx', axis=0, tiled=True)  43.8 us
    all_gather x1, waiting for transfers between devices, shards(): lax.all_gather(queries, 'ctx', axis=0, tiled=True)  38.3 us
    dot_general x20, matrix products, block_stats(): jnp.dot(weights.astype(jnp.bfloat16), values, preferred_element_type=jnp....  23.3 us
    dot_general x20, matrix products, block_stats(): jnp.einsum('rd,kd->rk', rows_q, key_rows, preferred_element_type=jnp.floa...  19.5 us
    dot_general x1, matrix products, shards(): jnp.dot(lax.all_gather(attended, 'ctx', axis=0, tiled=True), out_weight,...  9.45 us
    unnamed x17, local copies, waits for them, and re-layouts  8.42 us
    all_to_all x1, waiting for transfers between devices, shards(): lax.all_to_all(prefix_total[None], 'ctx', split_axis=2, concat_axis=0, ti...  5.55 us
  transfers between devices with their start and end apart: 5, of which 4 were waited for; matrix products, arithmetic and copies ran while one was open for 5% of the time, Pallas kernels for 0%

commit v1 on v0

v1 whole, which is shorter than its diff:
```python
import functools
import math

import jax
import jax.numpy as jnp
from jax import lax
from jax.experimental import pallas as pl
from jax.experimental.pallas import tpu as pltpu
from jax.sharding import PartitionSpec as P

HQ = 64
KVH = 4
HD = 128
CORES = 2
YN = 2
PAD = 16
STAT = 16
LOW = -1e30
LOG2E = math.log2(math.e)

F32 = jnp.float32
BF16 = jnp.bfloat16


def pack_partial(o, lse):
    hi = lse.astype(BF16).astype(F32)
    mid = (lse - hi).astype(BF16).astype(F32)
    lo = lse - hi - mid
    row = lax.broadcasted_iota(jnp.int32, (STAT, o.shape[1]), 0)
    stat = jnp.where(row == 0, hi, jnp.where(row == 1, mid, lo))
    return jnp.concatenate([o.astype(BF16), stat.astype(BF16)], axis=0)


def unpack_partial(packet):
    stat = packet[HD : HD + STAT].astype(F32)
    return packet[:HD].astype(F32), stat[0:1] + stat[1:2] + stat[2:3]


def merge_partials(parts):
    top = functools.reduce(jnp.maximum, [lse for _, lse in parts])
    weights = [jnp.exp2(lse - top) for _, lse in parts]
    total = functools.reduce(jnp.add, weights)
    inverse = 1.0 / total
    out = functools.reduce(
        jnp.add, [o * (w * inverse) for (o, _), w in zip(parts, weights)]
    )
    return out, top + jnp.log(total) * LOG2E


def kernel(
    n,
    positions,
    lengths,
    q_ref,
    nk_ref,
    cache,
    weight,
    att_out,
    proj_out,
    wv,
    kvx,
    vt,
    nkx,
    qd,
    qall,
    sc,
    pk,
    ry,
    zm,
    rz,
    ag,
    a_ref,
    acc,
    w_sem,
    kv_sem,
    kvs_sem,
    kvr_sem,
    nk_sem,
    nks_sem,
    nkr_sem,
    qd_sem,
    qds_sem,
    qdr_sem,
    qz_s,
    qz_r,
    qy_s,
    qy_r,
    ry_s,
    ry_r,
    rz_s,
    rz_r,
    gz_s,
    gz_r,
    gy_s,
    gy_r,
    gc_s,
    gc_r,
):
    zn = n // (YN * CORES)
    me = lax.axis_index("ctx")
    c = lax.rem(me, CORES)
    chip = me // CORES
    y = lax.rem(chip, YN)
    z = chip // YN
    oc = 1 - c
    oy = 1 - y
    jn = KVH // CORES
    per = HQ // KVH
    td = q_ref.shape[0]
    ct = td * CORES
    rows = per * ct
    lanes = YN * rows
    slots = cache.shape[0]
    gw = 2 * HD
    half = HQ // CORES * HD
    wide = per * HD
    ch = min(512, slots)
    units = jn * zn
    c2 = LOG2E / math.sqrt(HD)

    def zat(d):
        return lax.rem(z + d, zn)

    def zsrc(d):
        return lax.rem(z - d + zn, zn)

    def dev(zz, yy, cc):
        return {"ctx": (zz * YN + yy) * CORES + cc}

    peer = dev(z, y, oc)
    ypart = dev(z, oy, c)

    def remote(src, dst, ssem, rsem, target):
        return pltpu.make_async_remote_copy(
            src_ref=src,
            dst_ref=dst,
            send_sem=ssem,
            recv_sem=rsem,
            device_id=target,
            device_id_type=pl.DeviceIdType.MESH,
        )

    def arrived(slot, sem):
        pltpu.make_async_copy(slot, slot, sem).wait()

    def cols(group):
        return pl.ds(pl.multiple_of(group * gw, gw), gw)

    local = []
    for j in range(jn):
        local.append(
            pltpu.make_async_copy(cache.at[:, cols(c * jn + j)], kvx.at[j, c], kv_sem.at[j])
        )
    for j in range(jn):
        local.append(
            pltpu.make_async_copy(nk_ref.at[:, cols(c * jn + j)], nkx.at[j, c], nk_sem.at[j])
        )
    q_half = pl.ds(pl.multiple_of(c * half, half), half)
    q_other = pl.ds(pl.multiple_of(oc * half, half), half)
    q_local = pltpu.make_async_copy(q_ref.at[:, q_half], qd.at[c], qd_sem)
    q_local.start()
    for copy in local:
        copy.start()

    barrier = pltpu.get_barrier_semaphore()
    pl.semaphore_signal(barrier, inc=1, device_id=peer, device_id_type=pl.DeviceIdType.MESH)
    pl.semaphore_signal(barrier, inc=1, device_id=ypart, device_id_type=pl.DeviceIdType.MESH)
    for d in range(1, zn):
        pl.semaphore_signal(
            barrier, inc=1, device_id=dev(zat(d), y, c), device_id_type=pl.DeviceIdType.MESH
        )
    pl.semaphore_wait(barrier, zn + 1)

    sends = []

    def send(*args):
        copy = remote(*args)
        copy.start()
        sends.append(copy)

    send(q_ref.at[:, q_other], qd.at[c], qds_sem, qdr_sem, peer)
    for j in range(jn):
        send(nk_ref.at[:, cols(oc * jn + j)], nkx.at[j, c], nks_sem.at[j], nkr_sem.at[j], peer)
        send(cache.at[:, cols(oc * jn + j)], kvx.at[j, c], kvs_sem.at[j], kvr_sem.at[j], peer)
    weights = []
    for j in range(jn):
        for k in range(CORES):
            g = k * jn + j
            copy = pltpu.make_async_copy(
                weight.at[pl.ds(g * wide, wide), :], wv.at[g], w_sem.at[g]
            )
            copy.start()
            weights.append(copy)

    q_local.wait()
    arrived(qd.at[oc], qdr_sem)
    my_rows = pl.ds(pl.multiple_of(y * rows, rows), rows)
    other_rows = pl.ds(pl.multiple_of(oy * rows, rows), rows)
    for j in range(jn):
        tiles = []
        for h in range(per):
            at = (j * per + h) * HD
            tiles.append(
                jnp.concatenate(
                    [qd[k, :, at : at + HD].astype(F32) for k in range(CORES)], axis=0
                )
            )
        qall[z, j, my_rows, :] = jnp.concatenate(tiles, axis=0).astype(BF16)

    mine = qall.at[z, :, my_rows]
    send(mine, mine, qy_s.at[0], qy_r.at[0], ypart)
    for d in range(1, zn):
        send(mine, mine, qz_s.at[d], qz_r.at[d], dev(zat(d), y, c))

    for j in range(jn):
        local[j].wait()
        local[jn + j].wait()
        arrived(nkx.at[j, oc], nkr_sem.at[j])
        arrived(kvx.at[j, oc], kvr_sem.at[j])
        for k in range(CORES):
            vt[j, k] = kvx[j, k, :, HD:].T
    arrived(qall.at[z, :, other_rows], qy_r.at[0])

    def attend(j, d):
        zz = zsrc(d)
        q = qall[zz, j]
        lane = lax.broadcasted_iota(jnp.int32, (1, lanes), 1)
        token = lax.rem(lane, ct) + (lane // rows) * ct
        pos = jnp.zeros((1, lanes), jnp.int32)
        for t in range(YN * ct):
            pos = jnp.where(token == t, positions[zz * (YN * ct) + t], pos)
        top = jnp.full((8, lanes), LOW, F32)
        for k in range(CORES):
            live = lengths[chip * CORES + k]
            for i in range(slots // ch):
                s = lax.dot_general(
                    kvx[j, k, i * ch : (i + 1) * ch, :HD],
                    q,
                    (((1,), (1,)), ((), ())),
                    preferred_element_type=F32,
                )
                slot = lax.broadcasted_iota(jnp.int32, s.shape, 0)
                s = jnp.where(slot < live - i * ch, s, LOW)
                top = jnp.maximum(top, jnp.max(s.reshape(ch // 8, 8, lanes), axis=0))
                at = k * slots + i * ch
                sc[at : at + ch, :] = s
        row = lax.broadcasted_iota(jnp.int32, (PAD, lanes), 0)
        fresh = []
        for k in range(CORES):
            s = lax.dot_general(
                nkx[j, k, :, :HD], q, (((1,), (1,)), ((), ())), preferred_element_type=F32
            )
            key_pos = jnp.full((PAD, lanes), jnp.int32(2**30))
            for t in range(td):
                key_pos = jnp.where(row == t, positions[chip * ct + k * td + t], key_pos)
            s = jnp.where(pos >= key_pos, s, LOW)
            top = jnp.maximum(top, jnp.max(s.reshape(PAD // 8, 8, lanes), axis=0))
            fresh.append(s)
        high = jnp.max(top, axis=0, keepdims=True) * c2
        total = jnp.zeros((8, lanes), F32)
        out = jnp.zeros((HD, lanes), F32)
        for k in range(CORES):
            for i in range(slots // ch):
                at = k * slots + i * ch
                p = jnp.exp2(sc[at : at + ch, :] * c2 - high)
                total = total + jnp.sum(p.reshape(ch // 8, 8, lanes), axis=0)
                out = out + jnp.dot(
                    vt[j, k, :, i * ch : (i + 1) * ch],
                    p.astype(BF16),
                    preferred_element_type=F32,
                )
        for k in range(CORES):
            p = jnp.exp2(fresh[k] * c2 - high)
            total = total + jnp.sum(p.reshape(PAD // 8, 8, lanes), axis=0)
            out = out + lax.dot_general(
                nkx[j, k, :, HD:],
                p.astype(BF16),
                (((0,), (0,)), ((), ())),
                preferred_element_type=F32,
            )
        ell = jnp.sum(total, axis=0, keepdims=True)
        packet = pack_partial(out * (1.0 / ell), high + jnp.log(ell) * LOG2E)
        u = j * zn + d
        for yy in range(YN):
            pk[u, yy] = packet[:, yy * rows : (yy + 1) * rows]
        to_partner(u).start()

    def to_partner(u):
        return remote(pk.at[u, oy], ry.at[u], ry_s.at[u], ry_r.at[u], ypart)

    def to_owner(u, d):
        return remote(zm.at[u], rz.at[u], rz_s.at[u], rz_r.at[u], dev(zsrc(d), y, c))

    def fold(j, d):
        u = j * zn + d
        arrived(ry.at[u], ry_r.at[u])
        packet = pack_partial(
            *merge_partials([unpack_partial(pk[u, y]), unpack_partial(ry[u])])
        )

        @pl.when(d == 0)
        def _():
            rz[u] = packet

        @pl.when(d != 0)
        def _():
            zm[u] = packet
            to_owner(u, d).start()

    def relay_queries():
        for d in range(1, zn):
            slot = qall.at[zsrc(d), :, my_rows]
            arrived(slot, qz_r.at[d])
            send(slot, slot, qy_s.at[d], qy_r.at[d], ypart)

    def finish(j):
        for d in range(1, zn):
            arrived(rz.at[j * zn + d], rz_r.at[j * zn + d])
        out, _ = merge_partials([unpack_partial(rz[j * zn + d]) for d in range(zn)])
        out = out.T
        for h in range(per):
            ag[c, j, chip, :, h * HD : (h + 1) * HD] = out[h * ct : (h + 1) * ct].astype(BF16)
        slot = ag.at[c, j, chip]
        for d in range(1, zn):
            send(slot, slot, gz_s.at[j, d], gz_r.at[j, d], dev(zat(d), y, c))
        send(slot, slot, gy_s.at[j, 0], gy_r.at[j, 0], ypart)
        send(slot, slot, gc_s.at[j, 0, 0], gc_r.at[j, 0, 0], peer)

    def relay_outputs(j):
        for d in range(1, zn):
            slot = ag.at[c, j, zsrc(d) * YN + y]
            arrived(slot, gz_r.at[j, d])
            send(slot, slot, gy_s.at[j, d], gy_r.at[j, d], ypart)
            send(slot, slot, gc_s.at[j, 0, d], gc_r.at[j, 0, d], peer)
        for d in range(zn):
            slot = ag.at[c, j, zsrc(d) * YN + oy]
            arrived(slot, gy_r.at[j, d])
            send(slot, slot, gc_s.at[j, 1, d], gc_r.at[j, 1, d], peer)

    def project(j):
        for d in range(zn):
            arrived(ag.at[oc, j, zsrc(d) * YN + y], gc_r.at[j, 0, d])
            arrived(ag.at[oc, j, zsrc(d) * YN + oy], gc_r.at[j, 1, d])
        width = proj_out.shape[1]
        nb = min(256, width)
        for k in range(CORES):
            g = k * jn + j
            weights[j * CORES + k].wait()
            whole = jnp.concatenate(
                [ag[k, j, i].astype(F32) for i in range(zn * YN)], axis=0
            )
            a_ref[k] = whole.astype(BF16)
            own = ag[k, j, chip].astype(F32)
            own = jnp.where(c == 0, own[:td], own[td:])
            att_out[:, g * wide : (g + 1) * wide] = own.astype(BF16)

        def column(i, carry):
            at = pl.ds(pl.multiple_of(i * nb, nb), nb)
            part = jnp.dot(a_ref[0], wv[j, :, at], preferred_element_type=F32)
            for k in range(1, CORES):
                part = part + jnp.dot(
                    a_ref[k], wv[k * jn + j, :, at], preferred_element_type=F32
                )
            if j > 0:
                part = part + acc[:, at]
            if j == jn - 1:
                proj_out[:, at] = part.astype(BF16)
            else:
                acc[:, at] = part
            return carry

        lax.fori_loop(0, width // nb, column, 0)

    def step(u, carry):
        j = u // zn
        d = lax.rem(u, zn)

        @pl.when((u > 0) & (u < zn))
        def _():
            slot = qall.at[zsrc(d), :, other_rows]
            arrived(slot, qy_r.at[d])

        attend(j, d)

        @pl.when(u > 0)
        def _():
            fold((u - 1) // zn, lax.rem(u - 1, zn))

        return carry

    lax.fori_loop(0, 1, step, 0)
    relay_queries()
    lax.fori_loop(1, units, step, 0)
    fold(jn - 1, zn - 1)
    for j in range(jn):
        finish(j)
    for j in range(jn):
        relay_outputs(j)
    for j in range(jn):
        project(j)

    for copy in sends:
        copy.wait_send()

    def drain(u, carry):
        to_partner(u).wait_send()
        d = lax.rem(u, zn)

        @pl.when(d != 0)
        def _():
            to_owner(u, d).wait_send()

        return carry

    lax.fori_loop(0, units, drain, 0)


def shards(queries, new_kv, prefix_cache, positions, lengths, out_weight):
    n = lax.axis_size("ctx")
    td = queries.shape[0]
    zn = n // (YN * CORES)
    jn = KVH // CORES
    per = HQ // KVH
    ct = td * CORES
    rows = per * ct
    slots = prefix_cache.shape[0]
    width = out_weight.shape[1]
    wide = per * HD
    units = jn * zn
    dma = pltpu.SemaphoreType.DMA
    scratch = [
        pltpu.VMEM((KVH, wide, width), BF16),
        pltpu.VMEM((jn, CORES, slots, 2 * HD), BF16),
        pltpu.VMEM((jn, CORES, HD, slots), BF16),
        pltpu.VMEM((jn, CORES, PAD, 2 * HD), BF16),
        pltpu.VMEM((CORES, td, HQ // CORES * HD), BF16),
        pltpu.VMEM((zn, jn, YN * rows, HD), BF16),
        pltpu.VMEM((CORES * slots, YN * rows), F32),
        pltpu.VMEM((units, YN, HD + STAT, rows), BF16),
        pltpu.VMEM((units, HD + STAT, rows), BF16),
        pltpu.VMEM((units, HD + STAT, rows), BF16),
        pltpu.VMEM((units, HD + STAT, rows), BF16),
        pltpu.VMEM((CORES, jn, zn * YN, ct, wide), BF16),
        pltpu.VMEM((CORES, td * n, wide), BF16),
        pltpu.VMEM((td * n, width), F32),
        dma((KVH,)),
        dma((jn,)),
        dma((jn,)),
        dma((jn,)),
        dma((jn,)),
        dma((jn,)),
        dma((jn,)),
        dma,
        dma,
        dma,
        dma((zn,)),
        dma((zn,)),
        dma((zn,)),
        dma((zn,)),
        dma((units,)),
        dma((units,)),
        dma((units,)),
        dma((units,)),
        dma((jn, zn)),
        dma((jn, zn)),
        dma((jn, zn)),
        dma((jn, zn)),
        dma((jn, YN, zn)),
        dma((jn, YN, zn)),
    ]
    padded = jnp.pad(new_kv, ((0, PAD - td), (0, 0)))
    smem = pl.BlockSpec(memory_space=pltpu.SMEM)
    vmem = pl.BlockSpec(memory_space=pltpu.VMEM)
    hbm = pl.BlockSpec(memory_space=pl.ANY)
    return pl.pallas_call(
        functools.partial(kernel, n),
        out_shape=(
            jax.ShapeDtypeStruct(queries.shape, BF16),
            jax.ShapeDtypeStruct((td * n, width), BF16),
        ),
        in_specs=[smem, smem, vmem, vmem, hbm, hbm],
        out_specs=(vmem, vmem),
        scratch_shapes=scratch,
        compiler_params=pltpu.CompilerParams(
            collective_id=0,
            has_side_effects=True,
            vmem_limit_bytes=60 * 2**20,
        ),
        name="turn_attention",
    )(positions, lengths, queries, padded, prefix_cache, out_weight)


def solution(mesh):
    in_specs = (
        P(("groups", "ctx"), None),
        P(("groups", "ctx"), None),
        P(("groups", "ctx"), None),
        P("groups"),
        P("groups"),
        P(None, "ctx"),
    )
    out_specs = (P(("groups", "ctx"), None), P("groups", "ctx"))
    return jax.shard_map(shards, mesh=mesh, in_specs=in_specs, out_specs=out_specs, check_vma=False)
```

time: 249 us -> 57.2 us (0.23)
  waiting for transfers between devices: 93.1 us -> 0 us
  matrix products: 52.2 us -> 0 us
  Pallas kernels: 0 us -> 51.9 us
  blocking collectives: 50.6 us -> 0 us
  between operations: 14.4 us -> 0.64 us
  local copies, waits for them, and re-layouts: 15.5 us -> 4.38 us
  starting transfers between devices: 11 us -> 0 us
  other arithmetic: 9.62 us -> 0 us
    all_gather x2 -> x0, waiting for transfers between devices: 82.1 us -> none  [the longest x1 43.8 us: shards(): lax.all_gather(attended, 'ctx', axis=0, tiled=True)]
    dot_general x41 -> x0, matrix products: 52.2 us -> none  [the longest x20 23.3 us: block_stats(): jnp.dot(weights.astype(jnp.bfloat16), values, preferred_element_type=jnp....]
    pallas_call x0 -> x1, Pallas kernels: none -> 51.9 us  [shards(): pl.pallas_call(functools.partial(kernel, n), out_shape=(jax.ShapeDtypeStr...]
    all_gather x1 -> x0, blocking collectives: 50.6 us -> none  [shards(): lax.all_gather(new_kv, 'ctx', axis=0, tiled=True)]
    all_to_all x3 -> x0, starting transfers between devices: 10.9 us -> none  [the longest x1 3.72 us: shards(): lax.all_to_all(prefix_sum[None], 'ctx', split_axis=2, concat_axis=0, tile...]
    all_to_all x3 -> x0, waiting for transfers between devices: 10.4 us -> none  [the longest x1 5.55 us: shards(): lax.all_to_all(prefix_total[None], 'ctx', split_axis=2, concat_axis=0, ti...]
    unnamed x17 -> x2, local copies, waits for them, and re-layouts: 8.42 us -> 3.06 us
    reduce_sum x7 -> x0, other arithmetic: 3.98 us -> none  [the longest x5 3.19 us: block_stats(): row_total = jnp.sum(weights, axis=1)]
  transfers between devices with their start and end apart: 5 -> 0, of which waited for: 4 -> 0; matrix products, arithmetic and copies ran while one was open for 5% -> 0% of each run, Pallas kernels for 0% -> 0%
where the time goes in v1:
time: 57.2 us; the launch traced here: 56.9 us
  Pallas kernels  51.9 us (91%)
  local copies, waits for them, and re-layouts  4.38 us (8%)
  between operations  0.64 us (1%)
    pallas_call x1, Pallas kernels, shards(): pl.pallas_call(functools.partial(kernel, n), out_shape=(jax.ShapeDtypeStr...  51.9 us
    unnamed x2, local copies, waits for them, and re-layouts  3.06 us
    pad x1, local copies, waits for them, and re-layouts, shards(): padded = jnp.pad(new_kv, ((0, PAD - td), (0, 0)))  1.32 us

profile of v1, /device:TPU:0, one launch (start us, length us, event | category | flops | bytes accessed | tf_op | source)
XLA Modules:
  0.0 56.9 jit_solution(2902312720845313294)
XLA Ops:
  0.6 1.3 %pad.4.nk_ref = bf16[16,1024]{1,0:T(8,128)(2,1)} pad(bf16[4,1024]{1,0:T(4,128)(2,1)} %param.7, bf16[]{:T(256)} %constant.2.clone.1), padding=0_12x0_0 | pad | bytes 40962 | tf_op jit(solution)/shard_map/jit(_pad)/pad | solution.py:471
  1.9 51.9 %turn_attention.1 = (bf16[4,8192]{1,0:T(4,128)(2,1)}, bf16[64,1024]{1,0:T(8,128)(2,1)}) custom-call(s32[64]{0:T(128)} %positions.1, s32[16]{0:T(128)} %lengths.1, bf16[4,8192]{1,0:T(4,128)(2,1)} %q_ref.1, bf16[16,1024]{1,0:T(8,128)(2,1)} %pad.4.nk_ref, bf16[1024,1024]{1,0:T(8,128)(2,1)} %cache.1, bf16[8192,1024]{1,0:T(8,128)(2,1)} %weight.1), custom_call_target="tpu_custom_call" | custom-call | tf_op jit(solution)/shard_map/turn_attention/pallas_call | solution.py:475
  53.8 1.5 %copy.10 = bf16[4,8192]{1,0:T(4,128)(2,1)} copy(bf16[4,8192]{1,0:T(4,128)(2,1)} %get-tuple-element.4) | data formatting | bytes 131072
  55.3 1.6 %copy.11 = bf16[64,1024]{1,0:T(8,128)(2,1)} copy(bf16[64,1024]{1,0:T(8,128)(2,1)} %get-tuple-element.5) | data formatting | bytes 262144

commit v2 on v1

--- a/solution.py
+++ b/solution.py
@@ -61,6 +61,7 @@
     kvx,
     vt,
     nkx,
+    nkp,
     qd,
     qall,
     sc,
@@ -119,10 +120,18 @@
     c2 = LOG2E / math.sqrt(HD)
 
     def zat(d):
-        return lax.rem(z + d, zn)
+        if zn & (zn - 1):
+            return lax.rem(z + d, zn)
+        out = 0
+        for bit in range(zn.bit_length() - 1):
+            step = 1 << bit
+            out = out + lax.rem(z // step + d // step, 2) * step
+        return out
 
     def zsrc(d):
-        return lax.rem(z - d + zn, zn)
+        if zn & (zn - 1):
+            return lax.rem(z - d + zn, zn)
+        return zat(d)
 
     def dev(zz, yy, cc):
         return {"ctx": (zz * YN + yy) * CORES + cc}
@@ -216,10 +225,12 @@
         local[j].wait()
         local[jn + j].wait()
         arrived(nkx.at[j, oc], nkr_sem.at[j])
+        fresh = [nkx[j, k].astype(F32) for k in range(CORES)]
+        fresh.append(jnp.zeros((PAD - ct, gw), F32))
+        nkp[j] = jnp.concatenate(fresh, axis=0).astype(BF16)
         arrived(kvx.at[j, oc], kvr_sem.at[j])
         for k in range(CORES):
             vt[j, k] = kvx[j, k, :, HD:].T
-    arrived(qall.at[z, :, other_rows], qy_r.at[0])
 
     def attend(j, d):
         zz = zsrc(d)
@@ -245,17 +256,14 @@
                 at = k * slots + i * ch
                 sc[at : at + ch, :] = s
         row = lax.broadcasted_iota(jnp.int32, (PAD, lanes), 0)
-        fresh = []
-        for k in range(CORES):
-            s = lax.dot_general(
-                nkx[j, k, :, :HD], q, (((1,), (1,)), ((), ())), preferred_element_type=F32
-            )
-            key_pos = jnp.full((PAD, lanes), jnp.int32(2**30))
-            for t in range(td):
-                key_pos = jnp.where(row == t, positions[chip * ct + k * td + t], key_pos)
-            s = jnp.where(pos >= key_pos, s, LOW)
-            top = jnp.maximum(top, jnp.max(s.reshape(PAD // 8, 8, lanes), axis=0))
-            fresh.append(s)
+        fresh = lax.dot_general(
+            nkp[j, :, :HD], q, (((1,), (1,)), ((), ())), preferred_element_type=F32
+        )
+        key_pos = jnp.full((PAD, lanes), jnp.int32(2**30))
+        for t in range(ct):
+            key_pos = jnp.where(row == t, positions[chip * ct + t], key_pos)
+        fresh = jnp.where(pos >= key_pos, fresh, LOW)
+        top = jnp.maximum(top, jnp.max(fresh.reshape(PAD // 8, 8, lanes), axis=0))
         high = jnp.max(top, axis=0, keepdims=True) * c2
         total = jnp.zeros((8, lanes), F32)
         out = jnp.zeros((HD, lanes), F32)
@@ -269,15 +277,14 @@
                     p.astype(BF16),
                     preferred_element_type=F32,
                 )
-        for k in range(CORES):
-            p = jnp.exp2(fresh[k] * c2 - high)
-            total = total + jnp.sum(p.reshape(PAD // 8, 8, lanes), axis=0)
-            out = out + lax.dot_general(
-                nkx[j, k, :, HD:],
-                p.astype(BF16),
-                (((0,), (0,)), ((), ())),
-                preferred_element_type=F32,
-            )
+        p = jnp.exp2(fresh * c2 - high)
+        total = total + jnp.sum(p.reshape(PAD // 8, 8, lanes), axis=0)
+        out = out + lax.dot_general(
+            nkp[j, :, HD:],
+            p.astype(BF16),
+            (((0,), (0,)), ((), ())),
+            preferred_element_type=F32,
+        )
         ell = jnp.sum(total, axis=0, keepdims=True)
         packet = pack_partial(out * (1.0 / ell), high + jnp.log(ell) * LOG2E)
         u = j * zn + d
@@ -298,6 +305,10 @@
             *merge_partials([unpack_partial(pk[u, y]), unpack_partial(ry[u])])
         )
 
+        if isinstance(d, int) and d == 0:
+            rz[u] = packet
+            return
+
         @pl.when(d == 0)
         def _():
             rz[u] = packet
@@ -307,11 +318,13 @@
             zm[u] = packet
             to_owner(u, d).start()
 
-    def relay_queries():
-        for d in range(1, zn):
-            slot = qall.at[zsrc(d), :, my_rows]
-            arrived(slot, qz_r.at[d])
-            send(slot, slot, qy_s.at[d], qy_r.at[d], ypart)
+    def query_relay(d):
+        slot = qall.at[zsrc(d), :, my_rows]
+        return remote(slot, slot, qy_s.at[d], qy_r.at[d], ypart)
+
+    def relay_query(d):
+        arrived(qall.at[zsrc(d), :, my_rows], qz_r.at[d])
+        query_relay(d).start()
 
     def finish(j):
         for d in range(1, zn):
@@ -326,44 +339,35 @@
         send(slot, slot, gy_s.at[j, 0], gy_r.at[j, 0], ypart)
         send(slot, slot, gc_s.at[j, 0, 0], gc_r.at[j, 0, 0], peer)
 
-    def relay_outputs(j):
+    def relay_along(j):
         for d in range(1, zn):
             slot = ag.at[c, j, zsrc(d) * YN + y]
             arrived(slot, gz_r.at[j, d])
             send(slot, slot, gy_s.at[j, d], gy_r.at[j, d], ypart)
             send(slot, slot, gc_s.at[j, 0, d], gc_r.at[j, 0, d], peer)
+
+    def relay_across(j):
         for d in range(zn):
             slot = ag.at[c, j, zsrc(d) * YN + oy]
             arrived(slot, gy_r.at[j, d])
             send(slot, slot, gc_s.at[j, 1, d], gc_r.at[j, 1, d], peer)
 
-    def project(j):
-        for d in range(zn):
-            arrived(ag.at[oc, j, zsrc(d) * YN + y], gc_r.at[j, 0, d])
-            arrived(ag.at[oc, j, zsrc(d) * YN + oy], gc_r.at[j, 1, d])
+    def project(j, k, first, last):
         width = proj_out.shape[1]
         nb = min(256, width)
-        for k in range(CORES):
-            g = k * jn + j
-            weights[j * CORES + k].wait()
-            whole = jnp.concatenate(
-                [ag[k, j, i].astype(F32) for i in range(zn * YN)], axis=0
-            )
-            a_ref[k] = whole.astype(BF16)
-            own = ag[k, j, chip].astype(F32)
-            own = jnp.where(c == 0, own[:td], own[td:])
-            att_out[:, g * wide : (g + 1) * wide] = own.astype(BF16)
+        g = k * jn + j
+        whole = jnp.concatenate([ag[k, j, i].astype(F32) for i in range(zn * YN)], axis=0)
+        a_ref[...] = whole.astype(BF16)
+        own = ag[k, j, chip].astype(F32)
+        own = jnp.where(c == 0, own[:td], own[td:])
+        att_out[:, pl.ds(pl.multiple_of(g * wide, wide), wide)] = own.astype(BF16)
 
         def column(i, carry):
             at = pl.ds(pl.multiple_of(i * nb, nb), nb)
-            part = jnp.dot(a_ref[0], wv[j, :, at], preferred_element_type=F32)
-            for k in range(1, CORES):
-                part = part + jnp.dot(
-                    a_ref[k], wv[k * jn + j, :, at], preferred_element_type=F32
-                )
-            if j > 0:
+            part = jnp.dot(a_ref[...], wv[g, :, at], preferred_element_type=F32)
+            if not first:
                 part = part + acc[:, at]
-            if j == jn - 1:
+            if last:
                 proj_out[:, at] = part.astype(BF16)
             else:
                 acc[:, at] = part
@@ -371,33 +375,64 @@
 
         lax.fori_loop(0, width // nb, column, 0)
 
-    def step(u, carry):
-        j = u // zn
-        d = lax.rem(u, zn)
-
-        @pl.when((u > 0) & (u < zn))
-        def _():
-            slot = qall.at[zsrc(d), :, other_rows]
-            arrived(slot, qy_r.at[d])
-
-        attend(j, d)
-
-        @pl.when(u > 0)
-        def _():
-            fold((u - 1) // zn, lax.rem(u - 1, zn))
+    def project_both(j):
+        if j == 0:
+            for copy in weights:
+                copy.wait()
+        project(j, c, j == 0, False)
+        for d in range(zn):
+            arrived(ag.at[oc, j, zsrc(d) * YN + y], gc_r.at[j, 0, d])
+            arrived(ag.at[oc, j, zsrc(d) * YN + oy], gc_r.at[j, 1, d])
+        project(j, oc, False, j == jn - 1)
+
+    relay_query(1)
+    arrived(qall.at[z, :, other_rows], qy_r.at[0])
+    attend(0, 0)
+    relay_query(2)
+    attend(1, 0)
+    for d in range(3, zn):
+        relay_query(d)
+
+    def first_group(d, carry):
+        arrived(qall.at[zsrc(d), :, other_rows], qy_r.at[d])
+        attend(0, d)
+
+        @pl.when(d >= 2)
+        def _():
+            fold(0, d - 2)
 
         return carry
 
-    lax.fori_loop(0, 1, step, 0)
-    relay_queries()
-    lax.fori_loop(1, units, step, 0)
-    fold(jn - 1, zn - 1)
-    for j in range(jn):
-        finish(j)
-    for j in range(jn):
-        relay_outputs(j)
-    for j in range(jn):
-        project(j)
+    def second_group(d, carry):
+        attend(1, d)
+
+        @pl.when(d == 1)
+        def _():
+            fold(0, zn - 2)
+            fold(0, zn - 1)
+
+        @pl.when(d == 2)
+        def _():
+            fold(1, 0)
+
+        @pl.when(d >= 3)
+        def _():
+            fold(1, d - 2)
+
+        return carry
+
+    lax.fori_loop(1, zn, first_group, 0)
+    lax.fori_loop(1, zn, second_group, 0)
+    finish(0)
+    fold(1, zn - 2)
+    fold(1, zn - 1)
+    relay_along(0)
+    finish(1)
+    relay_across(0)
+    relay_along(1)
+    project_both(0)
+    relay_across(1)
+    project_both(1)
 
     for copy in sends:
         copy.wait_send()
@@ -409,6 +444,10 @@
         @pl.when(d != 0)
         def _():
             to_owner(u, d).wait_send()
+
+        @pl.when((u > 0) & (u < zn))
+        def _():
+            query_relay(d).wait_send()
 
         return carry
 
@@ -432,7 +471,8 @@
         pltpu.VMEM((KVH, wide, width), BF16),
         pltpu.VMEM((jn, CORES, slots, 2 * HD), BF16),
         pltpu.VMEM((jn, CORES, HD, slots), BF16),
-        pltpu.VMEM((jn, CORES, PAD, 2 * HD), BF16),
+        pltpu.VMEM((jn, CORES, td, 2 * HD), BF16),
+        pltpu.VMEM((jn, PAD, 2 * HD), BF16),
         pltpu.VMEM((CORES, td, HQ // CORES * HD), BF16),
         pltpu.VMEM((zn, jn, YN * rows, HD), BF16),
         pltpu.VMEM((CORES * slots, YN * rows), F32),
@@ -441,7 +481,7 @@
         pltpu.VMEM((units, HD + STAT, rows), BF16),
         pltpu.VMEM((units, HD + STAT, rows), BF16),
         pltpu.VMEM((CORES, jn, zn * YN, ct, wide), BF16),
-        pltpu.VMEM((CORES, td * n, wide), BF16),
+        pltpu.VMEM((td * n, wide), BF16),
         pltpu.VMEM((td * n, width), F32),
         dma((KVH,)),
         dma((jn,)),
@@ -468,7 +508,6 @@
         dma((jn, YN, zn)),
         dma((jn, YN, zn)),
     ]
-    padded = jnp.pad(new_kv, ((0, PAD - td), (0, 0)))
     smem = pl.BlockSpec(memory_space=pltpu.SMEM)
     vmem = pl.BlockSpec(memory_space=pltpu.VMEM)
     hbm = pl.BlockSpec(memory_space=pl.ANY)
@@ -487,7 +526,7 @@
             vmem_limit_bytes=60 * 2**20,
         ),
         name="turn_attention",
-    )(positions, lengths, queries, padded, prefix_cache, out_weight)
+    )(positions, lengths, queries, new_kv, prefix_cache, out_weight)
 
 
 def solution(mesh):

time: 57.2 us -> 50.6 us (0.88)
  Pallas kernels: 51.9 us -> 46.7 us
  local copies, waits for them, and re-layouts: 4.38 us -> 3.06 us
    pallas_call x1, Pallas kernels: 51.9 us -> 46.7 us  [shards(): pl.pallas_call(functools.partial(kernel, n), out_shape=(jax.ShapeDtypeStr...]
    pad x1 -> x0, local copies, waits for them, and re-layouts: 1.32 us -> none  [shards(): padded = jnp.pad(new_kv, ((0, PAD - td), (0, 0)))]
where the time goes in v2:
time: 50.6 us; the launch traced here: 50.4 us
  Pallas kernels  46.7 us (92%)
  local copies, waits for them, and re-layouts  3.06 us (6%)
  between operations  0.64 us (1%)
    pallas_call x1, Pallas kernels, shards(): pl.pallas_call(functools.partial(kernel, n), out_shape=(jax.ShapeDtypeStr...  46.7 us
    unnamed x2, local copies, waits for them, and re-layouts  3.06 us

profile of v2, /device:TPU:0, one launch (start us, length us, event | category | flops | bytes accessed | tf_op | source)
XLA Modules:
  0.0 50.4 jit_solution(13482057850216592677)
XLA Ops:
  0.6 46.7 %turn_attention.1 = (bf16[4,8192]{1,0:T(4,128)(2,1)}, bf16[64,1024]{1,0:T(8,128)(2,1)}) custom-call(s32[64]{0:T(128)} %positions.1, s32[16]{0:T(128)} %lengths.1, bf16[4,8192]{1,0:T(4,128)(2,1)} %q_ref.1, bf16[4,1024]{1,0:T(4,128)(2,1)} %nk_ref.1, bf16[1024,1024]{1,0:T(8,128)(2,1)} %cache.1, bf16[8192,1024]{1,0:T(8,128)(2,1)} %weight.1), custom_call_target="tpu_custom_call" | custom-call | tf_op jit(solution)/shard_map/turn_attention/pallas_call | solution.py:514
  47.3 1.5 %copy.10 = bf16[4,8192]{1,0:T(4,128)(2,1)} copy(bf16[4,8192]{1,0:T(4,128)(2,1)} %get-tuple-element.4) | data formatting | bytes 131072
  48.8 1.6 %copy.11 = bf16[64,1024]{1,0:T(8,128)(2,1)} copy(bf16[64,1024]{1,0:T(8,128)(2,1)} %get-tuple-element.5) | data formatting | bytes 262144

commit v3 on v2

--- a/solution.py
+++ b/solution.py
@@ -216,10 +216,12 @@
             )
         qall[z, j, my_rows, :] = jnp.concatenate(tiles, axis=0).astype(BF16)
 
-    mine = qall.at[z, :, my_rows]
-    send(mine, mine, qy_s.at[0], qy_r.at[0], ypart)
-    for d in range(1, zn):
-        send(mine, mine, qz_s.at[d], qz_r.at[d], dev(zat(d), y, c))
+    for j in range(jn):
+        mine = qall.at[z, j, my_rows]
+        send(mine, mine, qy_s.at[j, 0], qy_r.at[j, 0], ypart)
+        for i in range(1, zn):
+            d = zn - i if j else i
+            send(mine, mine, qz_s.at[j, d], qz_r.at[j, d], dev(zat(d), y, c))
 
     for j in range(jn):
         local[j].wait()
@@ -318,13 +320,16 @@
             zm[u] = packet
             to_owner(u, d).start()
 
-    def query_relay(d):
-        slot = qall.at[zsrc(d), :, my_rows]
-        return remote(slot, slot, qy_s.at[d], qy_r.at[d], ypart)
-
-    def relay_query(d):
-        arrived(qall.at[zsrc(d), :, my_rows], qz_r.at[d])
-        query_relay(d).start()
+    def query_relay(j, d):
+        slot = qall.at[zsrc(d), j, my_rows]
+        return remote(slot, slot, qy_s.at[j, d], qy_r.at[j, d], ypart)
+
+    def relay_query(j, d):
+        arrived(qall.at[zsrc(d), j, my_rows], qz_r.at[j, d])
+        query_relay(j, d).start()
+
+    def query_wait(j, d):
+        arrived(qall.at[zsrc(d), j, other_rows], qy_r.at[j, d])
 
     def finish(j):
         for d in range(1, zn):
@@ -339,15 +344,15 @@
         send(slot, slot, gy_s.at[j, 0], gy_r.at[j, 0], ypart)
         send(slot, slot, gc_s.at[j, 0, 0], gc_r.at[j, 0, 0], peer)
 
-    def relay_along(j):
-        for d in range(1, zn):
+    def relay_along(j, start, stop):
+        for d in range(start, stop):
             slot = ag.at[c, j, zsrc(d) * YN + y]
             arrived(slot, gz_r.at[j, d])
             send(slot, slot, gy_s.at[j, d], gy_r.at[j, d], ypart)
             send(slot, slot, gc_s.at[j, 0, d], gc_r.at[j, 0, d], peer)
 
-    def relay_across(j):
-        for d in range(zn):
+    def relay_across(j, start, stop):
+        for d in range(start, stop):
             slot = ag.at[c, j, zsrc(d) * YN + oy]
             arrived(slot, gy_r.at[j, d])
             send(slot, slot, gc_s.at[j, 1, d], gc_r.at[j, 1, d], peer)
@@ -375,26 +380,23 @@
 
         lax.fori_loop(0, width // nb, column, 0)
 
-    def project_both(j):
-        if j == 0:
-            for copy in weights:
-                copy.wait()
-        project(j, c, j == 0, False)
+    def project_peer(j):
         for d in range(zn):
             arrived(ag.at[oc, j, zsrc(d) * YN + y], gc_r.at[j, 0, d])
             arrived(ag.at[oc, j, zsrc(d) * YN + oy], gc_r.at[j, 1, d])
         project(j, oc, False, j == jn - 1)
 
-    relay_query(1)
-    arrived(qall.at[z, :, other_rows], qy_r.at[0])
+    relay_query(0, 1)
+    query_wait(0, 0)
     attend(0, 0)
-    relay_query(2)
+    for d in range(2, zn):
+        relay_query(0, d)
+    query_wait(1, 0)
     attend(1, 0)
-    for d in range(3, zn):
-        relay_query(d)
 
     def first_group(d, carry):
-        arrived(qall.at[zsrc(d), :, other_rows], qy_r.at[d])
+        relay_query(1, zn - d)
+        query_wait(0, d)
         attend(0, d)
 
         @pl.when(d >= 2)
@@ -404,7 +406,8 @@
         return carry
 
     def second_group(d, carry):
-        attend(1, d)
+        query_wait(1, zn - d)
+        attend(1, zn - d)
 
         @pl.when(d == 1)
         def _():
@@ -417,22 +420,28 @@
 
         @pl.when(d >= 3)
         def _():
-            fold(1, d - 2)
+            fold(1, zn - (d - 2))
 
         return carry
 
     lax.fori_loop(1, zn, first_group, 0)
     lax.fori_loop(1, zn, second_group, 0)
+    for copy in weights:
+        copy.wait()
     finish(0)
-    fold(1, zn - 2)
-    fold(1, zn - 1)
-    relay_along(0)
+    fold(1, 2)
+    fold(1, 1)
+    relay_along(0, 1, zn)
     finish(1)
-    relay_across(0)
-    relay_along(1)
-    project_both(0)
-    relay_across(1)
-    project_both(1)
+    relay_across(0, 0, zn)
+    relay_along(1, 1, zn - 1)
+    project(0, c, True, False)
+    relay_along(1, zn - 1, zn)
+    relay_across(1, 0, zn - 1)
+    project_peer(0)
+    relay_across(1, zn - 1, zn)
+    project(1, c, False, False)
+    project_peer(1)
 
     for copy in sends:
         copy.wait_send()
@@ -445,9 +454,7 @@
         def _():
             to_owner(u, d).wait_send()
 
-        @pl.when((u > 0) & (u < zn))
-        def _():
-            query_relay(d).wait_send()
+            query_relay(u // zn, d).wait_send()
 
         return carry
 
@@ -493,10 +500,10 @@
         dma,
         dma,
         dma,
-        dma((zn,)),
-        dma((zn,)),
-        dma((zn,)),
-        dma((zn,)),
+        dma((jn, zn)),
+        dma((jn, zn)),
+        dma((jn, zn)),
+        dma((jn, zn)),
         dma((units,)),
         dma((units,)),
         dma((units,)),

time: 50.6 us -> 48.7 us (0.962)
  Pallas kernels: 46.7 us -> 44.8 us
    pallas_call x1, Pallas kernels: 46.7 us -> 44.8 us  [shards(): pl.pallas_call(functools.partial(kernel, n), out_shape=(jax.ShapeDtypeStr...]
where the time goes in v3:
time: 48.7 us; the launch traced here: 48.5 us
  Pallas kernels  44.8 us (92%)
  local copies, waits for them, and re-layouts  3.06 us (6%)
  between operations  0.64 us (1%)
    pallas_call x1, Pallas kernels, shards(): pl.pallas_call(functools.partial(kernel, n), out_shape=(jax.ShapeDtypeStr...  44.8 us
    unnamed x2, local copies, waits for them, and re-layouts  3.06 us

profile of v3, /device:TPU:0, one launch (start us, length us, event | category | flops | bytes accessed | tf_op | source)
XLA Modules:
  0.0 48.5 jit_solution(2324824063417237925)
XLA Ops:
  0.6 44.8 %turn_attention.1 = (bf16[4,8192]{1,0:T(4,128)(2,1)}, bf16[64,1024]{1,0:T(8,128)(2,1)}) custom-call(s32[64]{0:T(128)} %positions.1, s32[16]{0:T(128)} %lengths.1, bf16[4,8192]{1,0:T(4,128)(2,1)} %q_ref.1, bf16[4,1024]{1,0:T(4,128)(2,1)} %nk_ref.1, bf16[1024,1024]{1,0:T(8,128)(2,1)} %cache.1, bf16[8192,1024]{1,0:T(8,128)(2,1)} %weight.1), custom_call_target="tpu_custom_call" | custom-call | tf_op jit(solution)/shard_map/turn_attention/pallas_call | solution.py:521
  45.4 1.5 %copy.10 = bf16[4,8192]{1,0:T(4,128)(2,1)} copy(bf16[4,8192]{1,0:T(4,128)(2,1)} %get-tuple-element.4) | data formatting | bytes 131072
  46.9 1.6 %copy.11 = bf16[64,1024]{1,0:T(8,128)(2,1)} copy(bf16[64,1024]{1,0:T(8,128)(2,1)} %get-tuple-element.5) | data formatting | bytes 262144

commit v4 on v3

--- a/solution.py
+++ b/solution.py
@@ -461,6 +461,11 @@
     lax.fori_loop(0, units, drain, 0)
 
 
+def hand_over(att, proj, att_out, proj_out):
+    att_out[...] = att[...]
+    proj_out[...] = proj[...]
+
+
 def shards(queries, new_kv, prefix_cache, positions, lengths, out_weight):
     n = lax.axis_size("ctx")
     td = queries.shape[0]
@@ -518,7 +523,7 @@
     smem = pl.BlockSpec(memory_space=pltpu.SMEM)
     vmem = pl.BlockSpec(memory_space=pltpu.VMEM)
     hbm = pl.BlockSpec(memory_space=pl.ANY)
-    return pl.pallas_call(
+    results = pl.pallas_call(
         functools.partial(kernel, n),
         out_shape=(
             jax.ShapeDtypeStruct(queries.shape, BF16),
@@ -534,6 +539,13 @@
         ),
         name="turn_attention",
     )(positions, lengths, queries, new_kv, prefix_cache, out_weight)
+    return pl.pallas_call(
+        hand_over,
+        out_shape=tuple(jax.ShapeDtypeStruct(r.shape, r.dtype) for r in results),
+        in_specs=[vmem, vmem],
+        out_specs=(vmem, vmem),
+        name="hand_over",
+    )(*results)
 
 
 def solution(mesh):

time: 48.7 us -> 47.2 us (0.969)
  local copies, waits for them, and re-layouts: 3.06 us -> 0 us
  Pallas kernels: 44.8 us -> 46.4 us
    unnamed x2 -> x0, local copies, waits for them, and re-layouts: 3.06 us -> none
    pallas_call x0 -> x1, Pallas kernels: none -> 1.63 us  [shards(): pl.pallas_call(hand_over, out_shape=tuple((jax.ShapeDtypeStruct(r.shape,...]
where the time goes in v4:
time: 47.2 us; the launch traced here: 47.1 us
  Pallas kernels  46.4 us (98%)
  between operations  0.64 us (1%)
    pallas_call x1, Pallas kernels, shards(): pl.pallas_call(functools.partial(kernel, n), out_shape=(jax.ShapeDtypeStr...  44.8 us
    pallas_call x1, Pallas kernels, shards(): pl.pallas_call(hand_over, out_shape=tuple((jax.ShapeDtypeStruct(r.shape,...  1.63 us

profile of v4, /device:TPU:0, one launch (start us, length us, event | category | flops | bytes accessed | tf_op | source)
XLA Modules:
  0.0 47.1 jit_solution(14857986561482197636)
XLA Ops:
  0.6 44.8 %turn_attention.1 = (bf16[4,8192]{1,0:T(4,128)(2,1)}, bf16[64,1024]{1,0:T(8,128)(2,1)}) custom-call(s32[64]{0:T(128)} %positions.1, s32[16]{0:T(128)} %lengths.1, bf16[4,8192]{1,0:T(4,128)(2,1)} %q_ref.1, bf16[4,1024]{1,0:T(4,128)(2,1)} %nk_ref.1, bf16[1024,1024]{1,0:T(8,128)(2,1)} %cache.1, bf16[8192,1024]{1,0:T(8,128)(2,1)} %weight.1), custom_call_target="tpu_custom_call" | custom-call | tf_op jit(solution)/shard_map/turn_attention/pallas_call | solution.py:526
  45.4 1.6 %hand_over.1 = (bf16[4,8192]{1,0:T(4,128)(2,1)}, bf16[64,1024]{1,0:T(8,128)(2,1)}) custom-call(bf16[4,8192]{1,0:T(4,128)(2,1)} %get-tuple-element.4.att, bf16[64,1024]{1,0:T(8,128)(2,1)} %get-tuple-element.5.proj), custom_call_target="tpu_custom_call" | custom-call | tf_op jit(solution)/shard_map/hand_over/pallas_call | solution.py:542
